TPU v7x, 128 devices: a whole 4x4x4 slice. The times are simulated.
128 devices in a mesh: ctx: 16 (over z, x_lo, core), tp: 8 (over x_hi, y).
Axes of the slice: x: 4 (x_hi: 2, x_lo: 2; x = x_hi * 2 + x_lo), y: 4, z: 4, core: 2. Of those that a mesh axis runs over, the one named last changes fastest.
Arguments:
- tokens: bfloat16 [2, 4096, 8192], P(None, 'ctx', 'tp'), may hold values from -14 to 14
- norm_gain: float32 [8192], replicated, may hold values from 0.5 to 1.5
- span_order: int32 [2, 32], replicated, may hold values from 0 to 31, each once within a row
- w_query: bfloat16 [8192, 4096], P('ctx', 'tp'), may hold values from -0.10122281 to 0.10122281
- w_key: bfloat16 [8192, 1024], P('ctx', 'tp'), may hold values from -0.10122281 to 0.10122281
- value_weight: bfloat16 [8192, 1024], P('ctx', 'tp'), may hold values from -0.0625 to 0.0625
- w_out: bfloat16 [4096, 8192], P('tp', 'ctx'), may hold values from -0.75 to 0.75
Outputs:
- mixed: bfloat16 [2, 4096, 8192], P(None, 'ctx', 'tp')
Inputs may be any that keep to these rules, and one draw needn't show every extreme that they name: Each row of span_order names every one of the 2 * 16 blocks of positions once; stored block b of a sequence holds positions span_order[b] * 128 onwards, in order.
All inputs are finite; a program needn't handle non-finite values.
Results may differ from a plain program's by a relative error of at most 0.014.
Values may be sent and summed in bfloat16 or wider, within the bound.
A program may use at most 128 MiB of HBM per device.

v0:
```python
import math
import jax
import jax.numpy as jnp
from jax import lax
from jax.sharding import PartitionSpec as P

HEAD_DIM = 128
theta_base = 500000.0
norm_eps = 1e-05
masked_score = -1e30


def in_one_piece(arrays, axis, dim, along):
    ends, at = ([], 0)
    for a in arrays[:-1]:
        at += a.shape[along]
        ends.append(at)
    both = jnp.concatenate(arrays, axis=along)
    return tuple(jnp.split(lax.all_gather(both, axis, axis=dim, tiled=True), ends, axis=along))


def normalize(flat_rows, norm_gain):
    wide = flat_rows.astype(jnp.float32)
    factor = lax.rsqrt(jnp.mean(wide * wide, axis=-1, keepdims=True) + norm_eps)
    return (wide * factor * norm_gain).astype(jnp.bfloat16)


def positions_of(span_order, first, count, block_rows):
    stored = first + jnp.arange(count, dtype=jnp.int32)
    which = stored // block_rows
    slots = jnp.arange(span_order.shape[1], dtype=jnp.int32)
    picked = jnp.sum(
        jnp.where(slots[None, None, :] == which[None, :, None], span_order[:, None, :], 0), axis=2
    )
    return picked * block_rows + stored % block_rows


def apply_rotation(value_rows, token_position, head_size):
    half = head_size // 2
    freqs = jnp.exp(-(2.0 * jnp.arange(half, dtype=jnp.float32) / head_size) * math.log(theta_base))
    angle = token_position.astype(jnp.float32)[..., None] * freqs
    cosine = jnp.cos(angle)[:, :, None, :]
    sine = jnp.sin(angle)[:, :, None, :]
    front = value_rows[..., :half]
    back = value_rows[..., half:]
    return jnp.concatenate([front * cosine - back * sine, back * cosine + front * sine], axis=-1)


def per_device(tokens, norm_gain, span_order, w_query, w_key, value_weight, w_out):
    sequence_batch, rows_dev, _ = tokens.shape
    head_size = HEAD_DIM
    query_heads = w_query.shape[1] // head_size
    key_heads = w_key.shape[1] // head_size
    group_width = query_heads // key_heads
    block_rows = rows_dev // 2
    total_rows = sequence_batch * rows_dev
    factor = 1.0 / math.sqrt(head_size)
    rank = lax.axis_index("ctx")
    whole = lax.all_gather(tokens, "tp", axis=2, tiled=True)
    normed = normalize(whole.reshape(total_rows, whole.shape[2]), norm_gain)
    query_pos = positions_of(span_order, rank * rows_dev, rows_dev, block_rows)
    latest = jnp.max(query_pos, axis=1)
    stat_shape = (sequence_batch, key_heads, group_width, rows_dev)
    initial = (
        jnp.full(stat_shape, masked_score, jnp.float32),
        jnp.zeros(stat_shape, jnp.float32),
        jnp.zeros(stat_shape + (head_size,), jnp.float32),
    )
    pieces = in_one_piece((w_query, w_key, value_weight), "ctx", 0, 1)
    query_flat, flattened_key, flattened_value = tuple(
        (jnp.dot(normed, piece, preferred_element_type=jnp.float32) for piece in pieces)
    )
    turned = apply_rotation(
        query_flat.reshape(sequence_batch, rows_dev, query_heads, head_size), query_pos, head_size
    ).astype(jnp.bfloat16)
    query = turned.reshape(sequence_batch, rows_dev, key_heads, group_width, head_size).transpose(
        0, 2, 3, 1, 4
    )
    turned = apply_rotation(
        flattened_key.reshape(sequence_batch, rows_dev, key_heads, head_size), query_pos, head_size
    ).astype(jnp.bfloat16)
    own_values = flattened_value.reshape(sequence_batch, rows_dev, key_heads, head_size).astype(
        jnp.bfloat16
    )
    key_piece, value_piece = in_one_piece((turned, own_values), "ctx", 1, 0)
    count = key_piece.shape[1]
    step_rows = 512

    def one_block(index, state):
        first = index * step_rows
        key_block = lax.dynamic_slice_in_dim(key_piece, first, step_rows, 1)
        value_block = lax.dynamic_slice_in_dim(value_piece, first, step_rows, 1)
        key_pos = positions_of(span_order, first, step_rows, block_rows)

        def update(current):
            peak, total, summed = current
            scores = (
                jnp.einsum(
                    "shgqd,skhd->shgqk", query, key_block, preferred_element_type=jnp.float32
                )
                * factor
            )
            allowed = key_pos[:, None, None, None, :] <= query_pos[:, None, None, :, None]
            scores = jnp.where(allowed, scores, masked_score)
            new_peak = jnp.maximum(peak, jnp.max(scores, axis=-1))
            weights = jnp.where(allowed, jnp.exp(scores - new_peak[..., None]), 0.0)
            shrink = jnp.exp(peak - new_peak)
            total = total * shrink + jnp.sum(weights, axis=-1)
            summed = summed * shrink[..., None] + jnp.einsum(
                "shgqk,skhd->shgqd",
                weights.astype(jnp.bfloat16),
                value_block,
                preferred_element_type=jnp.float32,
            )
            return (new_peak, total, summed)

        return lax.cond(
            jnp.all(jnp.min(key_pos, axis=1) > latest), lambda kept: kept, update, state
        )

    peak, total, summed = lax.fori_loop(0, count // step_rows, one_block, initial)
    attended = (summed / total[..., None]).astype(jnp.bfloat16)
    attended = attended.transpose(0, 3, 1, 2, 4).reshape(total_rows, query_heads * head_size)
    terms = jnp.dot(
        attended,
        lax.all_gather(w_out, "ctx", axis=1, tiled=True),
        preferred_element_type=jnp.float32,
    )
    mixed = lax.psum_scatter(terms.astype(jnp.bfloat16), "tp", scatter_dimension=1, tiled=True)
    return mixed.reshape(sequence_batch, rows_dev, mixed.shape[1])


def solution(mesh):
    placed = (
        P(None, "ctx", "tp"),
        P(),
        P(),
        P("ctx", "tp"),
        P("ctx", "tp"),
        P("ctx", "tp"),
        P("tp", "ctx"),
    )
    return jax.shard_map(
        per_device, mesh=mesh, in_specs=placed, out_specs=P(None, "ctx", "tp"), check_vma=False
    )
```

profile of v0, /device:TPU:0, one launch (start us, length us, event | category | flops | bytes accessed | tf_op | source)
XLA Modules:
  0.0 453.7 jit_solution(2648720766434171846)
XLA Ops:
  7.3 1.3 copy.28
  8.6 1.0 copy.29
  11.8 106.8 %all-gather.5.cloned.1.call-done = bf16[2,256,8192]{2,1,0:T(8,128)(2,1)} async-done(((bf16[2,256,1024]{2,1,0:T(8,128)(2,1)}), bf16[2,256,8192]{2,1,0:T(8,128)(2,1)}) %all-gather.5.cloned.1.call-update) | async-done | bytes 8388624 | tf_op jit(solution)/shard_map/all_gather | solution.py:59
  118.6 5.1 %fusion.27 = f32[2,256]{1,0:T(2,128)S(1)} fusion(bf16[2,256,8192]{2,1,0:T(8,128)(2,1)} %all-gather.5.cloned.1.call-done), kind=kLoop, calls=%fused_computation.41 | loop fusion | flops 12582400 | bytes 8390656 | tf_op jit(solution)/shard_map/reduce_sum | solution.py:24
  123.7 66.3 %all-gather.7.cloned.1.call-done = bf16[8192,768]{0,1:T(8,128)(2,1)} async-done(((bf16[512,768]{0,1:T(8,128)(2,1)}), bf16[8192,768]{0,1:T(8,128)(2,1)}) %all-gather.7.cloned.1.call-update) | async-done | bytes 12582928 | tf_op jit(solution)/shard_map/all_gather | solution.py:19
  190.0 7.0 %fusion.37 = f32[2,256,1,128]{1,3,0,2:T(8,128)S(1)} fusion(bf16[8192,768]{0,1:T(8,128)(2,1)} %all-gather.7.cloned.1.call-done, bf16[2,256,8192]{2,1,0:T(8,128)(2,1)} %all-gather.5.cloned.1.call-done, f32[8192]{0:T(1024)S(1)} %copy-done.1, f32[2,256]{1,0:T(2,128)S(1)} %add_rsqrt_fusion), kind=kOutput, calls=%fused_computation.51 | convolution fusion | flops 1090519040 | bytes 10782720 | tf_op jit(solution)/shard_map/dot_general | solution.py:71
  197.6 7.0 %fusion.43 = bf16[2,256,1,128]{1,3,0,2:T(8,128)(2,1)S(1)} fusion(bf16[8192,768]{0,1:T(8,128)(2,1)} %all-gather.7.cloned.1.call-done, bf16[2,256,8192]{2,1,0:T(8,128)(2,1)} %all-gather.5.cloned.1.call-done, f32[8192]{0:T(1024)S(1)} %copy-done.1, f32[2,256]{1,0:T(2,128)S(1)} %add_rsqrt_fusion), kind=kOutput, calls=%fused_computation.53 | convolution fusion | flops 1090584576 | bytes 10651648 | tf_op jit(solution)/shard_map/dot_general | solution.py:71
  206.8 7.7 %split.23 = bf16[8192,512]{0,1:T(8,128)(2,1)} slice(bf16[8192,768]{0,1:T(8,128)(2,1)} %all-gather.7.cloned.1.call-done), slice={[0:8192], [0:512]} | slice | bytes 16777216 | tf_op jit(solution)/shard_map/split | solution.py:19
  214.6 9.8 %fusion.30 = f32[2,256,4,128]{1,3,2,0:T(8,128)S(1)} fusion(bf16[4,128,8192,1]{2,1,0,3:T(8,128)(2,1)} %bitcast.90, bf16[2,256,8192]{2,1,0:T(8,128)(2,1)} %all-gather.5.cloned.1.call-done, f32[8192]{0:T(1024)S(1)} %copy-done.1, f32[2,256]{1,0:T(2,128)S(1)} %add_rsqrt_fusion), kind=kOutput, calls=%fused_computation.45 | convolution fusion | flops 4311744512 | bytes 17860608 | tf_op jit(solution)/shard_map/dot_general | solution.py:71
  224.8 26.8 %all-gather.9.cloned.1.call-done = bf16[4,4096,1,128]{1,3,0,2:T(8,128)(2,1)} async-done(((bf16[4,256,1,128]{1,3,0,2:T(8,128)(2,1)}), bf16[4,4096,1,128]{1,3,0,2:T(8,128)(2,1)}) %all-gather.9.cloned.1.call-update) | async-done | bytes 4194320 | tf_op jit(solution)/shard_map/all_gather | solution.py:19
  251.6 3.9 fusion.62
  255.5 4.1 copy.33
  259.6 2.4 copy.35
  262.1 59.5 %while.19 = (s32[]{:T(128)}, f32[2,1,4,256]{3,2,0,1:T(4,128)S(1)}, f32[2,1,4,256]{3,2,0,1:T(4,128)S(1)}, f32[2,1,4,256,128]{4,3,2,0,1:T(8,128)S(1)}, s32[2,32]{1...) while((s32[]{:T(128)}, f32[2,1,4,256]{3,2,0,1:T(4,128)S(1)}, ...), condition=%wide.region_11.12_spmd, body=%wide.region_3.11_spmd.sunk | while | flops 551389184 | bytes 16968260 | solution.py:121
  263.8 5.7 %conditional.2 = (f32[2,1,4,256]{3,2,0,1:T(4,128)S(1)}, f32[2,1,4,256]{3,2,0,1:T(4,128)S(1)}, f32[2,1,4,256,128]{4,3,2,0,1:T(8,128)S(1)}) conditional(s32[]{:T(128)} %convert_element_type.120, (s32[2,512]{1,0:T(2,128)S(1)}, s32[2,256]{1,0:T(2,128)S(1)}, s32[]{:T(128)}, bf16[2,4096,1,128]{3,1,0,2:T(8,128)(2,1)}, ...), branch_computations={%region_7.9_spmd, %region_10.10_spmd} | conditional | flops 551294976 | bytes 16898114 | solution.py:117
  264.0 1.8 fusion
  265.8 2.6 fusion.9
  268.4 1.0 fusion.2
  271.2 5.8 %conditional.2 = (f32[2,1,4,256]{3,2,0,1:T(4,128)S(1)}, f32[2,1,4,256]{3,2,0,1:T(4,128)S(1)}, f32[2,1,4,256,128]{4,3,2,0,1:T(8,128)S(1)}) conditional(s32[]{:T(128)} %convert_element_type.120, (s32[2,512]{1,0:T(2,128)S(1)}, s32[2,256]{1,0:T(2,128)S(1)}, s32[]{:T(128)}, bf16[2,4096,1,128]{3,1,0,2:T(8,128)(2,1)}, ...), branch_computations={%region_7.9_spmd, %region_10.10_spmd} | conditional | flops 551294976 | bytes 16898114 | solution.py:117
  271.4 1.8 fusion
  273.2 2.6 fusion.9
  275.9 1.0 fusion.2
  278.6 5.8 %conditional.2 = (f32[2,1,4,256]{3,2,0,1:T(4,128)S(1)}, f32[2,1,4,256]{3,2,0,1:T(4,128)S(1)}, f32[2,1,4,256,128]{4,3,2,0,1:T(8,128)S(1)}) conditional(s32[]{:T(128)} %convert_element_type.120, (s32[2,512]{1,0:T(2,128)S(1)}, s32[2,256]{1,0:T(2,128)S(1)}, s32[]{:T(128)}, bf16[2,4096,1,128]{3,1,0,2:T(8,128)(2,1)}, ...), branch_computations={%region_7.9_spmd, %region_10.10_spmd} | conditional | flops 551294976 | bytes 16898114 | solution.py:117
  278.9 1.8 fusion
  280.7 2.7 fusion.9
  283.3 1.0 fusion.2
  286.1 5.8 %conditional.2 = (f32[2,1,4,256]{3,2,0,1:T(4,128)S(1)}, f32[2,1,4,256]{3,2,0,1:T(4,128)S(1)}, f32[2,1,4,256,128]{4,3,2,0,1:T(8,128)S(1)}) conditional(s32[]{:T(128)} %convert_element_type.120, (s32[2,512]{1,0:T(2,128)S(1)}, s32[2,256]{1,0:T(2,128)S(1)}, s32[]{:T(128)}, bf16[2,4096,1,128]{3,1,0,2:T(8,128)(2,1)}, ...), branch_computations={%region_7.9_spmd, %region_10.10_spmd} | conditional | flops 551294976 | bytes 16898114 | solution.py:117
  286.3 1.8 fusion
  288.1 2.6 fusion.9
  290.8 1.0 fusion.2
  293.5 5.8 %conditional.2 = (f32[2,1,4,256]{3,2,0,1:T(4,128)S(1)}, f32[2,1,4,256]{3,2,0,1:T(4,128)S(1)}, f32[2,1,4,256,128]{4,3,2,0,1:T(8,128)S(1)}) conditional(s32[]{:T(128)} %convert_element_type.120, (s32[2,512]{1,0:T(2,128)S(1)}, s32[2,256]{1,0:T(2,128)S(1)}, s32[]{:T(128)}, bf16[2,4096,1,128]{3,1,0,2:T(8,128)(2,1)}, ...), branch_computations={%region_7.9_spmd, %region_10.10_spmd} | conditional | flops 551294976 | bytes 16898114 | solution.py:117
  293.8 1.8 fusion
  295.6 2.6 fusion.9
  298.2 1.0 fusion.2
  301.0 5.8 %conditional.2 = (f32[2,1,4,256]{3,2,0,1:T(4,128)S(1)}, f32[2,1,4,256]{3,2,0,1:T(4,128)S(1)}, f32[2,1,4,256,128]{4,3,2,0,1:T(8,128)S(1)}) conditional(s32[]{:T(128)} %convert_element_type.120, (s32[2,512]{1,0:T(2,128)S(1)}, s32[2,256]{1,0:T(2,128)S(1)}, s32[]{:T(128)}, bf16[2,4096,1,128]{3,1,0,2:T(8,128)(2,1)}, ...), branch_computations={%region_7.9_spmd, %region_10.10_spmd} | conditional | flops 551294976 | bytes 16898114 | solution.py:117
  301.2 1.8 fusion
  303.0 2.7 fusion.9
  305.7 1.0 fusion.2
  308.4 5.8 %conditional.2 = (f32[2,1,4,256]{3,2,0,1:T(4,128)S(1)}, f32[2,1,4,256]{3,2,0,1:T(4,128)S(1)}, f32[2,1,4,256,128]{4,3,2,0,1:T(8,128)S(1)}) conditional(s32[]{:T(128)} %convert_element_type.120, (s32[2,512]{1,0:T(2,128)S(1)}, s32[2,256]{1,0:T(2,128)S(1)}, s32[]{:T(128)}, bf16[2,4096,1,128]{3,1,0,2:T(8,128)(2,1)}, ...), branch_computations={%region_7.9_spmd, %region_10.10_spmd} | conditional | flops 551294976 | bytes 16898114 | solution.py:117
  308.7 1.8 fusion
  310.5 2.6 fusion.9
  313.1 1.0 fusion.2
  315.9 5.8 %conditional.2 = (f32[2,1,4,256]{3,2,0,1:T(4,128)S(1)}, f32[2,1,4,256]{3,2,0,1:T(4,128)S(1)}, f32[2,1,4,256,128]{4,3,2,0,1:T(8,128)S(1)}) conditional(s32[]{:T(128)} %convert_element_type.120, (s32[2,512]{1,0:T(2,128)S(1)}, s32[2,256]{1,0:T(2,128)S(1)}, s32[]{:T(128)}, bf16[2,4096,1,128]{3,1,0,2:T(8,128)(2,1)}, ...), branch_computations={%region_7.9_spmd, %region_10.10_spmd} | conditional | flops 551294976 | bytes 16898114 | solution.py:117
  316.1 1.8 fusion
  317.9 2.6 fusion.9
  320.5 1.0 fusion.2
  322.4 10.1 %convolution_convert_fusion = bf16[512,8192]{1,0:T(8,128)(2,1)} fusion(bf16[512,8192]{1,0:T(8,128)(2,1)} %all-gather.11.cloned.1.call-done, bf16[64,8,4,128]{3,2,1,0:T(4,128)(2,1)S(1)} %bitcast.93), kind=kOutput, calls=%fused_computation.44 | convolution fusion | flops 4299161600 | bytes 17301504 | tf_op jit(solution)/shard_map/dot_general | solution.py:124
  332.6 114.6 %reduce-scatter.2.cloned.1.call-done = bf16[512,1024]{1,0:T(8,128)(2,1)} async-done(((bf16[512,8192]{1,0:T(8,128)(2,1)}), bf16[512,1024]{1,0:T(8,128)(2,1)}) %reduce-scatter.2.cloned.1.call-update) | async-done | bytes 1048592 | tf_op jit(solution)/shard_map/reduce_scatter | solution.py:129
  (107 shorter events, 16.5 us)
Async XLA Ops:
  6.5 5.1 %copy-start = (s32[2,32]{1,0:T(2,128)S(1)}, s32[2,32]{1,0:T(2,128)}, u32[]{:S(2)}) copy-start(s32[2,32]{1,0:T(2,128)} %param.13) | copy-start | bytes 772
  6.5 112.1 %all-gather.5.cloned.1.call-start = ((), (), s32[]{:S(2)}) async-start(), calls=%async_computation.1 | async-start | bytes 9437184 | tf_op jit(solution)/shard_map/all_gather | solution.py:59
  7.3 182.8 %all-gather.7.cloned.1.call-start = ((), (), s32[]{:S(2)}) async-start(), calls=%async_computation.2 | async-start | bytes 13369344 | tf_op jit(solution)/shard_map/all_gather | solution.py:19
  11.5 240.1 %all-gather.9.cloned.1.call-start = ((), (), s32[]{:S(2)}) async-start(), calls=%async_computation.3 | async-start | bytes 4456448 | tf_op jit(solution)/shard_map/all_gather | solution.py:19
  11.8 178.3 %copy-start.1 = (f32[8192]{0:T(1024)S(1)}, f32[8192]{0:T(1024)}, u32[]{:S(2)}) copy-start(f32[8192]{0:T(1024)} %param.12) | copy-start | bytes 98308
  205.4 117.0 %all-gather.11.cloned.1.call-start = ((), (), s32[]{:S(2)}) async-start(), calls=%async_computation.4 | async-start | bytes 8912896 | tf_op jit(solution)/shard_map/all_gather | solution.py:126
  206.0 241.2 %reduce-scatter.2.cloned.1.call-start = ((), (), s32[]{:S(2)}) async-start(), calls=%async_computation.5 | async-start | bytes 9437184 | tf_op jit(solution)/shard_map/reduce_scatter | solution.py:129
Sparse Core Ops, SparseCore 0:
  9.6 108.9 all-gather.4
  120.3 69.7 all-gather.6
  205.5 46.0 all-gather.8
  253.1 52.2 all-gather.10
  332.7 114.4 reduce-scatter.1
where the time goes:
time: 455 us; the launch traced here: 454 us
  waiting for transfers between devices  316 us (69%)
  matrix products  69.2 us (15%)
  other arithmetic  26.5 us (6%)
  local copies, waits for them, and re-layouts  22.2 us (5%)
  between operations  13.3 us (3%)
  loops' own time  6.33 us (1%)
    reduce_scatter x1, waiting for transfers between devices, per_device(): lax.psum_scatter(terms.astype(jnp.bfloat16), 'tp', scatter_dimension=1, t...  115 us
    all_gather x1, waiting for transfers between devices, per_device(): whole = lax.all_gather(tokens, 'tp', axis=2, tiled=True)  107 us
    all_gather x2, waiting for transfers between devices, in_one_piece(): lax.all_gather(both, axis, axis=dim, tiled=True)  93.1 us
    dot_general x3, matrix products, per_device(): jnp.dot(normed, piece, preferred_element_type=jnp.float32)  23.8 us
    dot_general x8, matrix products, update(): jnp.einsum('shgqk,skhd->shgqd', weights.astype(jnp.bfloat16), value_block...  21.2 us
    dot_general x8, matrix products, update(): jnp.einsum('shgqd,skhd->shgqk', query, key_block, preferred_element_type=...  14.2 us
    split x2, local copies, waits for them, and re-layouts, in_one_piece(): jnp.split(lax.all_gather(both, axis, axis=dim, tiled=True), ends, axis=al...  11.6 us
    dot_general x1, matrix products, per_device(): jnp.dot(attended, lax.all_gather(w_out, 'ctx', axis=1, tiled=True), prefe...  10.1 us
  transfers between devices with their start and end apart: 5, of which 4 were waited for; matrix products, arithmetic and copies ran while one was open for 20% of the time, Pallas kernels for 0%

commit v1 on v0

--- a/solution.py
+++ b/solution.py
@@ -56,7 +56,8 @@
     total_rows = sequence_batch * rows_dev
     factor = 1.0 / math.sqrt(head_size)
     rank = lax.axis_index("ctx")
-    whole = lax.all_gather(tokens, "tp", axis=2, tiled=True)
+    parts = lax.all_gather(tokens, "tp", axis=0, tiled=False)
+    whole = jnp.concatenate(parts, axis=2)
     normed = normalize(whole.reshape(total_rows, whole.shape[2]), norm_gain)
     query_pos = positions_of(span_order, rank * rows_dev, rows_dev, block_rows)
     latest = jnp.max(query_pos, axis=1)

time: 455 us -> 464 us (1.020)
  waiting for transfers between devices: 316 us -> 269 us
  local copies, waits for them, and re-layouts: 22.2 us -> 60.4 us
  other arithmetic: 26.5 us -> 44.6 us
    all_gather x2, waiting for transfers between devices: 93.1 us -> 45.8 us  [in_one_piece(): lax.all_gather(both, axis, axis=dim, tiled=True)]
    convert_element_type x0 -> x2, local copies, waits for them, and re-layouts: none -> 25.7 us  [the longest x1 13.6 us: normalize(): return (wide * factor * norm_gain).astype(jnp.bfloat16)]
    unnamed x0 -> x2, other arithmetic: none -> 11.8 us
    mul x0 -> x2, local copies, waits for them, and re-layouts: none -> 11.3 us  [normalize(): return (wide * factor * norm_gain).astype(jnp.bfloat16)]
    mul x0 -> x1, other arithmetic: none -> 9.42 us  [normalize(): return (wide * factor * norm_gain).astype(jnp.bfloat16)]
  transfers between devices with their start and end apart: 5 -> 5, of which waited for: 4 -> 3; matrix products, arithmetic and copies ran while one was open for 20% -> 32% of each run, Pallas kernels for 0% -> 0%
where the time goes in v1:
time: 464 us; the launch traced here: 463 us
  waiting for transfers between devices  269 us (58%)
  matrix products  69.3 us (15%)
  local copies, waits for them, and re-layouts  60.4 us (13%)
  other arithmetic  44.6 us (10%)
  between operations  13.3 us (3%)
  loops' own time  5.96 us (1%)
    reduce_scatter x1, waiting for transfers between devices, per_device(): lax.psum_scatter(terms.astype(jnp.bfloat16), 'tp', scatter_dimension=1, t...  115 us
    all_gather x1, waiting for transfers between devices, per_device(): parts = lax.all_gather(tokens, 'tp', axis=0, tiled=False)  106 us
    all_gather x2, waiting for transfers between devices, in_one_piece(): lax.all_gather(both, axis, axis=dim, tiled=True)  45.8 us
    dot_general x3, matrix products, per_device(): jnp.dot(normed, piece, preferred_element_type=jnp.float32)  23.8 us
    dot_general x8, matrix products, update(): jnp.einsum('shgqk,skhd->shgqd', weights.astype(jnp.bfloat16), value_block...  21.2 us
    dot_general x8, matrix products, update(): jnp.einsum('shgqd,skhd->shgqk', query, key_block, preferred_element_type=...  14.2 us
    convert_element_type x1, local copies, waits for them, and re-layouts, normalize(): return (wide * factor * norm_gain).astype(jnp.bfloat16)  13.6 us
    convert_element_type x1, local copies, waits for them, and re-layouts, normalize(): wide = flat_rows.astype(jnp.float32)  12.1 us
  transfers between devices with their start and end apart: 5, of which 3 were waited for; matrix products, arithmetic and copies ran while one was open for 32% of the time, Pallas kernels for 0%

profile of v1, /device:TPU:0, one launch (start us, length us, event | category | flops | bytes accessed | tf_op | source)
XLA Modules:
  0.0 462.5 jit_solution(10028210709312620511)
XLA Ops:
  7.3 1.3 copy.45
  12.4 106.2 %all-gather.12.cloned.1.call-done = bf16[16,256,1024]{2,1,0:T(8,128)(2,1)} async-done(((bf16[2,256,1024]{2,1,0:T(8,128)(2,1)}), bf16[16,256,1024]{2,1,0:T(8,128)(2,1)}) %all-gather.12.cloned.1.call-update) | async-done | bytes 8388624 | tf_op jit(solution)/shard_map/all_gather | solution.py:59
  118.7 11.8 %convert_bitcast_fusion = f32[8,2,32,8,1024]{4,3,2,1,0:T(8,128)} fusion(bf16[16,256,1024]{2,1,0:T(8,128)(2,1)} %all-gather.12.cloned.1.call-done), kind=kLoop, calls=%fused_computation.41 | loop fusion | flops 4194304 | bytes 25165824
  130.4 12.1 %copy.62 = f32[8,2,32,8,1024]{4,3,0,2,1:T(8,128)} copy(f32[8,2,32,8,1024]{4,3,2,1,0:T(8,128)} %convert_bitcast_fusion) | data formatting | bytes 33554432 | tf_op jit(solution)/shard_map/convert_element_type | solution.py:23
  142.5 1.7 fusion.27
  144.3 45.8 %all-gather.6.cloned.1.call-done = bf16[8192,768]{0,1:T(8,128)(2,1)} async-done(((bf16[512,768]{0,1:T(8,128)(2,1)}), bf16[8192,768]{0,1:T(8,128)(2,1)}) %all-gather.6.cloned.1.call-update) | async-done | bytes 12582928 | tf_op jit(solution)/shard_map/all_gather | solution.py:19
  190.1 9.5 %fusion.35 = f32[2,256,1,128]{1,3,0,2:T(8,128)S(1)} fusion(bf16[8192,768]{0,1:T(8,128)(2,1)} %all-gather.6.cloned.1.call-done, f32[2,256,8192]{2,1,0:T(8,128)} %bitcast.100, f32[8192]{0:T(1024)S(1)} %copy-done.1, f32[2,256]{1,0:T(2,128)S(1)} %add_rsqrt_fusion), kind=kOutput, calls=%fused_computation.54 | convolution fusion | flops 1086324736 | bytes 19171328 | tf_op jit(solution)/shard_map/dot_general | solution.py:72
  201.2 4.8 %fusion.37 = bf16[2,256,1,128]{1,3,0,2:T(8,128)(2,1)S(1)} fusion(bf16[8192,768]{0,1:T(8,128)(2,1)} %all-gather.6.cloned.1.call-done, f32[2,256,8192]{2,1,0:T(8,128)S(1)} %bitcast.101, f32[8192]{0:T(1024)S(1)} %copy-done.1, f32[2,256]{1,0:T(2,128)S(1)} %add_rsqrt_fusion), kind=kOutput, calls=%fused_computation.56 | convolution fusion | flops 1086390272 | bytes 19040256 | tf_op jit(solution)/shard_map/dot_general | solution.py:72
  208.2 9.4 %fusion.30 = bf16[2,256,8,1024]{3,1,0,2:T(8,128)(2,1)} fusion(f32[8,1024]{1,0:T(8,128)S(1)} %mul.228, f32[2,256]{1,0:T(2,128)S(1)} %add_rsqrt_fusion, bf16[16,256,1024]{2,1,0:T(8,128)(2,1)} %all-gather.12.cloned.1.call-done), kind=kLoop, calls=%fused_computation.47 | loop fusion | flops 16777216 | bytes 16812032 | tf_op jit(solution)/shard_map/mul | solution.py:25
  217.6 11.3 %copy.50 = bf16[2,256,8,1024]{3,2,1,0:T(8,128)(2,1)} copy(bf16[2,256,8,1024]{3,1,0,2:T(8,128)(2,1)} %fusion.30) | data formatting | bytes 16777216 | tf_op jit(solution)/shard_map/mul | solution.py:25
  229.0 13.6 %reshape.362 = bf16[2,256,8192,1]{2,1,0,3:T(8,128)(2,1)} reshape(bf16[2,256,8,1024]{3,2,1,0:T(8,128)(2,1)} %copy.50) | data formatting | bytes 16777216 | tf_op jit(solution)/shard_map/convert_element_type | solution.py:25
  242.6 7.8 %split.23 = bf16[8192,512]{0,1:T(8,128)(2,1)} slice(bf16[8192,768]{0,1:T(8,128)(2,1)} %all-gather.6.cloned.1.call-done), slice={[0:8192], [0:512]} | slice | bytes 16777216 | tf_op jit(solution)/shard_map/split | solution.py:19
  250.4 9.5 %fusion.31 = f32[2,256,4,128]{1,3,2,0:T(8,128)S(1)} fusion(bf16[4,128,8192,1]{2,1,0,3:T(8,128)(2,1)} %bitcast.105, bf16[2,256,8192,1]{2,1,0,3:T(8,128)(2,1)} %reshape.362), kind=kOutput, calls=%fused_computation.48 | convolution fusion | flops 4294967296 | bytes 17825792 | tf_op jit(solution)/shard_map/dot_general | solution.py:72
  260.4 3.9 fusion.54
  264.4 4.1 copy.51
  268.4 2.5 copy.53
  271.0 58.9 %while.19 = (s32[]{:T(128)}, f32[2,1,4,256]{3,2,0,1:T(4,128)S(1)}, f32[2,1,4,256]{3,2,0,1:T(4,128)S(1)}, f32[2,1,4,256,128]{4,3,2,0,1:T(8,128)S(1)}, s32[2,32]{1...) while((s32[]{:T(128)}, f32[2,1,4,256]{3,2,0,1:T(4,128)S(1)}, ...), condition=%wide.region_11.12_spmd, body=%wide.region_3.11_spmd.sunk | while | flops 551389184 | bytes 16968260 | solution.py:122
  272.6 5.8 %conditional.2 = (f32[2,1,4,256]{3,2,0,1:T(4,128)S(1)}, f32[2,1,4,256]{3,2,0,1:T(4,128)S(1)}, f32[2,1,4,256,128]{4,3,2,0,1:T(8,128)S(1)}) conditional(s32[]{:T(128)} %convert_element_type.129, (s32[2,512]{1,0:T(2,128)S(1)}, s32[2,256]{1,0:T(2,128)S(1)}, s32[]{:T(128)}, bf16[2,4096,1,128]{3,1,0,2:T(8,128)(2,1)}, ...), branch_computations={%region_7.9_spmd, %region_10.10_spmd} | conditional | flops 551294976 | bytes 16898114 | solution.py:118
  272.8 1.8 fusion
  274.6 2.6 fusion.9
  277.3 1.0 fusion.2
  279.9 5.8 %conditional.2 = (f32[2,1,4,256]{3,2,0,1:T(4,128)S(1)}, f32[2,1,4,256]{3,2,0,1:T(4,128)S(1)}, f32[2,1,4,256,128]{4,3,2,0,1:T(8,128)S(1)}) conditional(s32[]{:T(128)} %convert_element_type.129, (s32[2,512]{1,0:T(2,128)S(1)}, s32[2,256]{1,0:T(2,128)S(1)}, s32[]{:T(128)}, bf16[2,4096,1,128]{3,1,0,2:T(8,128)(2,1)}, ...), branch_computations={%region_7.9_spmd, %region_10.10_spmd} | conditional | flops 551294976 | bytes 16898114 | solution.py:118
  280.2 1.8 fusion
  281.9 2.7 fusion.9
  287.3 5.8 %conditional.2 = (f32[2,1,4,256]{3,2,0,1:T(4,128)S(1)}, f32[2,1,4,256]{3,2,0,1:T(4,128)S(1)}, f32[2,1,4,256,128]{4,3,2,0,1:T(8,128)S(1)}) conditional(s32[]{:T(128)} %convert_element_type.129, (s32[2,512]{1,0:T(2,128)S(1)}, s32[2,256]{1,0:T(2,128)S(1)}, s32[]{:T(128)}, bf16[2,4096,1,128]{3,1,0,2:T(8,128)(2,1)}, ...), branch_computations={%region_7.9_spmd, %region_10.10_spmd} | conditional | flops 551294976 | bytes 16898114 | solution.py:118
  287.5 1.8 fusion
  289.4 2.6 fusion.9
  292.0 1.0 fusion.2
  294.7 5.8 %conditional.2 = (f32[2,1,4,256]{3,2,0,1:T(4,128)S(1)}, f32[2,1,4,256]{3,2,0,1:T(4,128)S(1)}, f32[2,1,4,256,128]{4,3,2,0,1:T(8,128)S(1)}) conditional(s32[]{:T(128)} %convert_element_type.129, (s32[2,512]{1,0:T(2,128)S(1)}, s32[2,256]{1,0:T(2,128)S(1)}, s32[]{:T(128)}, bf16[2,4096,1,128]{3,1,0,2:T(8,128)(2,1)}, ...), branch_computations={%region_7.9_spmd, %region_10.10_spmd} | conditional | flops 551294976 | bytes 16898114 | solution.py:118
  294.9 1.8 fusion
  296.7 2.6 fusion.9
  299.4 1.0 fusion.2
  302.1 5.7 %conditional.2 = (f32[2,1,4,256]{3,2,0,1:T(4,128)S(1)}, f32[2,1,4,256]{3,2,0,1:T(4,128)S(1)}, f32[2,1,4,256,128]{4,3,2,0,1:T(8,128)S(1)}) conditional(s32[]{:T(128)} %convert_element_type.129, (s32[2,512]{1,0:T(2,128)S(1)}, s32[2,256]{1,0:T(2,128)S(1)}, s32[]{:T(128)}, bf16[2,4096,1,128]{3,1,0,2:T(8,128)(2,1)}, ...), branch_computations={%region_7.9_spmd, %region_10.10_spmd} | conditional | flops 551294976 | bytes 16898114 | solution.py:118
  302.3 1.8 fusion
  304.1 2.6 fusion.9
  306.7 1.0 fusion.2
  309.4 5.7 %conditional.2 = (f32[2,1,4,256]{3,2,0,1:T(4,128)S(1)}, f32[2,1,4,256]{3,2,0,1:T(4,128)S(1)}, f32[2,1,4,256,128]{4,3,2,0,1:T(8,128)S(1)}) conditional(s32[]{:T(128)} %convert_element_type.129, (s32[2,512]{1,0:T(2,128)S(1)}, s32[2,256]{1,0:T(2,128)S(1)}, s32[]{:T(128)}, bf16[2,4096,1,128]{3,1,0,2:T(8,128)(2,1)}, ...), branch_computations={%region_7.9_spmd, %region_10.10_spmd} | conditional | flops 551294976 | bytes 16898114 | solution.py:118
  309.6 1.8 fusion
  311.4 2.6 fusion.9
  314.1 1.0 fusion.2
  316.7 5.7 %conditional.2 = (f32[2,1,4,256]{3,2,0,1:T(4,128)S(1)}, f32[2,1,4,256]{3,2,0,1:T(4,128)S(1)}, f32[2,1,4,256,128]{4,3,2,0,1:T(8,128)S(1)}) conditional(s32[]{:T(128)} %convert_element_type.129, (s32[2,512]{1,0:T(2,128)S(1)}, s32[2,256]{1,0:T(2,128)S(1)}, s32[]{:T(128)}, bf16[2,4096,1,128]{3,1,0,2:T(8,128)(2,1)}, ...), branch_computations={%region_7.9_spmd, %region_10.10_spmd} | conditional | flops 551294976 | bytes 16898114 | solution.py:118
  317.0 1.8 fusion
  318.8 2.6 fusion.9
  324.1 5.7 %conditional.2 = (f32[2,1,4,256]{3,2,0,1:T(4,128)S(1)}, f32[2,1,4,256]{3,2,0,1:T(4,128)S(1)}, f32[2,1,4,256,128]{4,3,2,0,1:T(8,128)S(1)}) conditional(s32[]{:T(128)} %convert_element_type.129, (s32[2,512]{1,0:T(2,128)S(1)}, s32[2,256]{1,0:T(2,128)S(1)}, s32[]{:T(128)}, bf16[2,4096,1,128]{3,1,0,2:T(8,128)(2,1)}, ...), branch_computations={%region_7.9_spmd, %region_10.10_spmd} | conditional | flops 551294976 | bytes 16898114 | solution.py:118
  324.3 1.8 fusion
  326.1 2.6 fusion.9
  330.7 10.1 %convolution_convert_fusion = bf16[512,8192]{1,0:T(8,128)(2,1)} fusion(bf16[512,8192]{1,0:T(8,128)(2,1)} %all-gather.10.cloned.1.call-done, bf16[64,8,4,128]{3,2,1,0:T(4,128)(2,1)S(1)} %bitcast.108), kind=kOutput, calls=%fused_computation.46 | convolution fusion | flops 4299161600 | bytes 17301504 | tf_op jit(solution)/shard_map/dot_general | solution.py:125
  340.7 115.3 %reduce-scatter.2.cloned.1.call-done = bf16[512,1024]{1,0:T(8,128)(2,1)} async-done(((bf16[512,8192]{1,0:T(8,128)(2,1)}), bf16[512,1024]{1,0:T(8,128)(2,1)}) %reduce-scatter.2.cloned.1.call-update) | async-done | bytes 1048592 | tf_op jit(solution)/shard_map/reduce_scatter | solution.py:130
  (120 shorter events, 22.1 us)
Async XLA Ops:
  6.5 112.1 %all-gather.12.cloned.1.call-start = ((), (), s32[]{:S(2)}) async-start(), calls=%async_computation.5 | async-start | bytes 9437184 | tf_op jit(solution)/shard_map/all_gather | solution.py:59
  7.3 182.8 %all-gather.6.cloned.1.call-start = ((), (), s32[]{:S(2)}) async-start(), calls=%async_computation.1 | async-start | bytes 13369344 | tf_op jit(solution)/shard_map/all_gather | solution.py:19
  11.5 248.9 %all-gather.8.cloned.1.call-start = ((), (), s32[]{:S(2)}) async-start(), calls=%async_computation.2 | async-start | bytes 4456448 | tf_op jit(solution)/shard_map/all_gather | solution.py:19
  118.7 23.9 %slice-start = ((s8[8388608]{0:T(1024)(128)(4,1)}), s8[4194304]{0:T(1024)(128)(4,1)S(1)}, s32[]{:S(2)}) async-start(s8[8388608]{0:T(1024)(128)(4,1)} %bitcast.102), calls=%async_computation.6 | async-start | bytes 8388608
  130.4 12.1 %slice-start.1 = ((s8[8388608]{0:T(1024)(128)(4,1)}), s8[4194304]{0:T(1024)(128)(4,1)S(1)}, s32[]{:S(2)}) async-start(s8[8388608]{0:T(1024)(128)(4,1)} %bitcast.102), calls=%async_computation.7 | async-start | bytes 8388608
  142.5 47.6 %copy-start.1 = (f32[8192]{0:T(1024)S(1)}, f32[8192]{0:T(1024)}, u32[]{:S(2)}) copy-start(f32[8192]{0:T(1024)} %param.12) | copy-start | bytes 98308
  190.1 11.1 %copy-start = (f32[8,2,32,8,1024]{4,3,0,2,1:T(8,128)S(1)}, f32[8,2,32,8,1024]{4,3,0,2,1:T(8,128)}, u32[]{:S(2)}) copy-start(f32[8,2,32,8,1024]{4,3,0,2,1:T(8,128)} %copy.62) | copy-start | bytes 50331652
  206.7 123.9 %all-gather.10.cloned.1.call-start = ((), (), s32[]{:S(2)}) async-start(), calls=%async_computation.3 | async-start | bytes 8912896 | tf_op jit(solution)/shard_map/all_gather | solution.py:127
  207.3 248.7 %reduce-scatter.2.cloned.1.call-start = ((), (), s32[]{:S(2)}) async-start(), calls=%async_computation.4 | async-start | bytes 9437184 | tf_op jit(solution)/shard_map/reduce_scatter | solution.py:130
  260.4 10.6 %copy-start.2 = (s32[2,32]{1,0:T(2,128)S(1)}, s32[2,32]{1,0:T(2,128)}, u32[]{:S(2)}) copy-start(s32[2,32]{1,0:T(2,128)} %param.13) | copy-start | bytes 772
Sparse Core Ops, SparseCore 0:
  9.7 108.9 all-gather.11
  120.3 69.7 all-gather.5
  206.9 46.0 all-gather.7
  254.5 52.2 all-gather.9
  340.9 115.0 reduce-scatter.1
